TPU v7x, 256 devices: a whole 4x4x8 slice. The times are simulated.
256 devices in a mesh: row: 8 (over x, core), col: 32 (over y, z).
Axes of the slice: x: 4, y: 4, z: 8, core: 2. Of those that a mesh axis runs over, the one named last changes fastest.
Arguments:
- embeddings: bfloat16 [32768, 512], P(('row', 'col')), may hold values from -6 to 6
- sketch: bfloat16 [32768, 64], P(('row', 'col')), may hold values from -240 to 240
Outputs:
- basis: float32 [32768, 64], P(('row', 'col'))
- first_pass: float32 [32768, 64], P(('row', 'col'))
All inputs are finite; a program needn't handle non-finite values.
Results may differ from a plain program's by a relative error of at most 0.00205.
Values may be sent and summed in bfloat16 or wider, within the bound.
A program may use at most 64 MiB of HBM per device.

v0:
```python
import jax
import jax.numpy as jnp
from jax import lax
from jax.sharding import Mesh
from jax.sharding import PartitionSpec as P

ROW = ("row_0", "row_1")
COL = ("col_0", "col_1")
ROW_COL = ("row_0", "row_1", "col_0", "col_1")


def in_order(blocks, dim):
    blocks = jnp.moveaxis(blocks, 0, dim)
    dims = blocks.shape
    return blocks.reshape(*dims[:dim], dims[dim] * dims[dim + 1], *dims[dim + 2 :])


def from_everyone(shard, axis):
    copies = jnp.broadcast_to(shard, (lax.axis_size(axis), *shard.shape))
    return lax.all_to_all(copies, axis, split_axis=0, concat_axis=0, tiled=True)


def gather_directly(shard, axis, dim):
    return in_order(from_everyone(shard, axis), dim)


def in_blocks(shard, dim, length):
    dims = shard.shape
    blocks = shard.reshape(*dims[:dim], length, dims[dim] // length, *dims[dim + 1 :])
    return jnp.moveaxis(blocks, dim, 0)


def sent_and_summed(shard, axis, dim):
    length = lax.axis_size(axis)
    blocks = lax.all_to_all(in_blocks(shard, dim, length), axis, 0, 0, tiled=True)
    return jnp.sum(blocks, axis=0)


def over_copies(shard, axis):
    return from_everyone(shard, axis).sum(axis=0)


def one_axis_at_a_time(shard, axes):
    far, near = axes
    return over_copies(over_copies(shard, near), far)


def squares_of(points):
    return jnp.sum(jnp.square(points.astype(jnp.float32)), axis=1)


def kernel_tile(left, right, left_sq, right_sq, gamma):
    cross = lax.dot_general(
        left, right, (((1,), (1,)), ((), ())), preferred_element_type=jnp.float32
    )
    dist = left_sq[:, None] + right_sq[None, :] - 2.0 * cross
    return jnp.exp(-gamma * dist).astype(jnp.bfloat16)


def product_of(left, right):
    return lax.dot_general(
        left,
        right,
        (((0,), (0,)), ((), ())),
        precision=lax.Precision.HIGHEST,
        preferred_element_type=jnp.float32,
    )


def per_device(embeddings, sketch):
    width = embeddings.shape[1]
    gamma = 3.0 / width
    own_points = gather_directly(embeddings, ROW, 0)
    own_sq = squares_of(own_points)
    empty = jnp.zeros((own_points.shape[0], sketch.shape[1]), jnp.float32)
    total = empty
    points = lax.all_gather(embeddings, COL, axis=0, tiled=True)
    tests = lax.all_gather(sketch, COL, axis=0, tiled=True)
    count = points.shape[0]
    size = 512

    def step(carry, block):
        block_points, block_tests = block
        tile = kernel_tile(own_points, block_points, own_sq, squares_of(block_points), gamma)
        return (carry + jnp.dot(tile, block_tests, preferred_element_type=jnp.float32), None)

    stacked = (
        points.reshape(count // size, size, width),
        tests.reshape(count // size, size, tests.shape[1]),
    )
    total, unused = lax.scan(step, total, stacked)
    sketched = sent_and_summed(total, ROW, 0)
    core = one_axis_at_a_time(
        product_of(sketch.astype(jnp.float32), sketched), (("row_0", "row_1"), ("col_0", "col_1"))
    )
    lower = jnp.linalg.cholesky(core)
    first = jax.scipy.linalg.solve_triangular(lower, sketched.T, lower=True).T
    gram_two = one_axis_at_a_time(
        product_of(first, first), (("row_0", "row_1"), ("col_0", "col_1"))
    )
    lower_two = jnp.linalg.cholesky(gram_two)
    second = jax.scipy.linalg.solve_triangular(lower_two, first.T, lower=True).T
    total_points = sketched.shape[0] * lax.axis_size(ROW) * lax.axis_size(COL)
    scale = jnp.sqrt(jnp.float32(total_points))
    return (second * scale, first * scale)


def solution(mesh):
    torus = Mesh(mesh.devices.reshape(4, 2, 4, 8), ("row_0", "row_1", "col_0", "col_1"))
    in_specs = (P(ROW_COL, None), P(ROW_COL, None))
    out_specs = (P(ROW_COL, None), P(ROW_COL, None))
    return jax.shard_map(
        per_device, mesh=torus, in_specs=in_specs, out_specs=out_specs, check_vma=False
    )
```

profile of v0, /device:TPU:1, one launch (start us, length us, event | category | flops | bytes accessed | tf_op | source)
XLA Modules:
  0.0 238.8 jit_solution(14531047242678938613)
XLA Ops:
  7.2 0.7 all-gather.2.cloned.1.call-update
  7.9 2.0 broadcast_in_dim.22
  9.9 6.7 %all-to-all-start = ((bf16[8,128,512]{2,1,0:T(8,128)(2,1)}), bf16[8,128,512]{2,1,0:T(8,128)(2,1)S(1)}, u32[]{:S(2)}, u32[]{:S(2)}) async-start(bf16[8,128,512]{2,1,0:T(8,128)(2,1)} %broadcast_in_dim.22), calls=%async_computation | async-start | bytes 2097152 | tf_op jit(solution)/shard_map/all_to_all | solution.py:20
  16.5 43.0 %all_gather.7 = bf16[4096,64]{0,1:T(8,128)(2,1)S(1)} all-gather(bf16[128,64]{0,1:T(8,128)(2,1)S(1)} %copy-done), channel_id=1, replica_groups=mesh['row_0'=4,'row_1'=2,'col_0'=4,'col_1'=8] {'col_0','col_1'}, dimensions={0}, use_global_device_ids=true | all-gather | bytes 540672 | tf_op jit(solution)/shard_map/all_gather | solution.py:78
  59.5 0.5 copy.19
  60.3 32.5 %all-gather.2.cloned.1.call-done = bf16[4096,512]{1,0:T(8,128)(2,1)} async-done(((bf16[128,512]{1,0:T(8,128)(2,1)}), bf16[4096,512]{1,0:T(8,128)(2,1)}) %all-gather.2.cloned.1.call-update) | async-done | bytes 4194320 | tf_op jit(solution)/shard_map/all_gather | solution.py:77
  92.8 26.7 %while.11 = (s32[]{:T(128)}, f32[1024,64]{0,1:T(8,128)S(1)}, f32[1024]{0:T(1024)S(1)}, bf16[8,512,512]{2,1,0:T(8,128)(2,1)}, bf16[1024,512]{1,0:T(8,128)(2,1)S(1...) while((s32[]{:T(128)}, f32[1024,64]{0,1:T(8,128)S(1)}, f32[1024]{0:T(1024)S(1)}, ...), condition=%wide.region_3.4_spmd.clone, body=%wide.region_1.3_spmd.clone.sunk | while | flops 607518208 | bytes 2761827 | solution.py:91
  92.8 1.2 multiply_reduce_fusion.3
  94.0 2.1 fusion.45
  96.1 1.2 multiply_reduce_fusion.3
  97.4 2.1 fusion.45
  99.5 1.2 multiply_reduce_fusion.3
  100.7 2.1 fusion.45
  102.8 1.2 multiply_reduce_fusion.3
  104.0 2.1 fusion.45
  106.1 1.2 multiply_reduce_fusion.3
  107.4 2.1 fusion.45
  109.5 1.2 multiply_reduce_fusion.3
  110.7 2.1 fusion.45
  112.8 1.2 multiply_reduce_fusion.3
  114.0 2.1 fusion.45
  116.1 1.2 multiply_reduce_fusion.3
  117.4 2.1 fusion.45
  119.5 14.7 %all_to_all.30 = f32[8,128,64]{1,2,0:T(8,128)S(1)} all-to-all(f32[8,128,64]{1,2,0:T(8,128)S(1)} %copy_bitcast_fusion), channel_id=1, replica_groups=mesh['row_0'=4,'row_1'=2,'col_0'=4,'col_1'=8] {'row_0','row_1'}, dimensions={0} | all-to-all | bytes 524288 | tf_op jit(solution)/shard_map/all_to_all | solution.py:35
  134.6 0.7 reshape.31
  135.3 19.0 %all_to_all.31 = f32[32,1,4096]{2,1,0:T(1,128)S(1)} all-to-all(f32[32,1,4096]{2,1,0:T(1,128)S(1)} %reshape.31), channel_id=1, replica_groups=mesh['row_0'=4,'row_1'=2,'col_0'=4,'col_1'=8] {'col_0','col_1'}, dimensions={0} | all-to-all | bytes 1048576 | tf_op jit(solution)/shard_map/all_to_all | solution.py:20
  154.3 0.5 broadcast.71
  154.8 1.9 reduce.5
  156.7 0.4 reshape.32
  157.4 11.4 %all_to_all.32 = f32[8,1,4096]{2,1,0:T(1,128)S(1)} all-to-all(f32[8,1,4096]{2,1,0:T(1,128)S(1)} %reshape.33), channel_id=1, replica_groups=mesh['row_0'=4,'row_1'=2,'col_0'=4,'col_1'=8] {'row_0','row_1'}, dimensions={0} | all-to-all | bytes 262144 | tf_op jit(solution)/shard_map/all_to_all | solution.py:20
  168.8 1.0 reduce.6
  170.0 5.8 %cholesky.44 = f32[64,64]{1,0:T(8,128)S(1)} custom-call(f32[64,64]{1,0:T(8,128)S(1)} %fusion.27), custom_call_target="Cholesky" | custom-call | tf_op jit(solution)/shard_map/jit(cholesky)/cholesky | solution.py:96
  175.9 0.6 compare_reduce_fusion.1
  176.5 0.7 fusion.20
  177.2 4.9 %custom-call.7 = f32[1,64,64]{1,2,0:T(8,128)S(1)} custom-call(f32[1,64,64]{2,1,0:T(8,128)S(1)} %fusion.20), custom_call_target="InvertDiagBlocksLowerTriangular" | custom-call | tf_op jit(solution)/shard_map/jit(_solve_triangular)/triangular_solve | solution.py:97
  182.6 0.7 reshape.35
  183.3 19.7 %all_to_all.33 = f32[32,1,4096]{2,1,0:T(1,128)S(1)} all-to-all(f32[32,1,4096]{2,1,0:T(1,128)S(1)} %reshape.35), channel_id=1, replica_groups=mesh['row_0'=4,'row_1'=2,'col_0'=4,'col_1'=8] {'col_0','col_1'}, dimensions={0} | all-to-all | bytes 1048576 | tf_op jit(solution)/shard_map/all_to_all | solution.py:20
  202.9 1.9 reduce.7
  205.4 0.8 reshape.37
  206.2 6.4 %all-to-all-start.5 = ((f32[8,1,4096]{2,1,0:T(1,128)}), f32[8,1,4096]{2,1,0:T(1,128)S(1)}, u32[]{:S(2)}, u32[]{:S(2)}) async-start(f32[8,1,4096]{2,1,0:T(1,128)} %reshape.37), calls=%async_computation.5 | async-start | bytes 262144 | tf_op jit(solution)/shard_map/all_to_all | solution.py:20
  212.6 0.6 multiply_bitcast_fusion
  213.2 4.6 %all-to-all-done.5 = f32[8,1,4096]{2,1,0:T(1,128)S(1)} async-done(((f32[8,1,4096]{2,1,0:T(1,128)}), f32[8,1,4096]{2,1,0:T(1,128)S(1)}, u32[]{:S(2)}, u32[]{:S(2)}) %all-to-all-start.5) | async-done | bytes 131104 | tf_op jit(solution)/shard_map/all_to_all | solution.py:20
  217.9 1.0 reduce.8
  219.0 5.8 %cholesky.55 = f32[64,64]{1,0:T(8,128)S(1)} custom-call(f32[64,64]{1,0:T(8,128)S(1)} %fusion.23), custom_call_target="Cholesky" | custom-call | tf_op jit(solution)/shard_map/jit(cholesky)/cholesky | solution.py:101
  224.9 0.6 compare_reduce_fusion
  225.6 0.7 fusion.21
  226.2 4.9 %custom-call.8 = f32[1,64,64]{1,2,0:T(8,128)S(1)} custom-call(f32[1,64,64]{2,1,0:T(8,128)S(1)} %fusion.21), custom_call_target="InvertDiagBlocksLowerTriangular" | custom-call | tf_op jit(solution)/shard_map/jit(_solve_triangular)/triangular_solve | solution.py:102
  231.1 0.9 fusion.19
  (30 shorter events, 2.5 us)
Async XLA Ops:
  7.2 9.4 %copy-start = (bf16[128,64]{0,1:T(8,128)(2,1)S(1)}, bf16[128,64]{0,1:T(8,128)(2,1)}, u32[]{:S(2)}) copy-start(bf16[128,64]{0,1:T(8,128)(2,1)} %param.8) | copy-start | bytes 49156
  7.2 85.6 %all-gather.2.cloned.1.call-start = ((), (), s32[]{:S(2)}) async-start(), calls=%async_computation.6 | async-start | bytes 4325376 | tf_op jit(solution)/shard_map/all_gather | solution.py:77
  9.9 50.1 %all-to-all-start = ((bf16[8,128,512]{2,1,0:T(8,128)(2,1)}), bf16[8,128,512]{2,1,0:T(8,128)(2,1)S(1)}, u32[]{:S(2)}, u32[]{:S(2)}) async-start(bf16[8,128,512]{2,1,0:T(8,128)(2,1)} %broadcast_in_dim.22), calls=%async_computation | async-start | bytes 2097152 | tf_op jit(solution)/shard_map/all_to_all | solution.py:20
  206.2 11.7 %all-to-all-start.5 = ((f32[8,1,4096]{2,1,0:T(1,128)}), f32[8,1,4096]{2,1,0:T(1,128)S(1)}, u32[]{:S(2)}, u32[]{:S(2)}) async-start(f32[8,1,4096]{2,1,0:T(1,128)} %reshape.37), calls=%async_computation.5 | async-start | bytes 262144 | tf_op jit(solution)/shard_map/all_to_all | solution.py:20
Sparse Core Ops, SparseCore 0:
  10.6 82.1 all-gather.1
where the time goes:
time: 240 us; the launch traced here: 239 us
  blocking collectives  108 us (45%)
  other arithmetic  40.7 us (17%)
  waiting for transfers between devices  37.8 us (16%)
  matrix products  18.2 us (8%)
  between operations  14.3 us (6%)
  starting transfers between devices  13.1 us (5%)
  local copies, waits for them, and re-layouts  6.8 us (3%)
    all_to_all x3, blocking collectives, from_everyone(): return lax.all_to_all(copies, axis, split_axis=0, concat_axis=0, tiled=True)  50 us
    all_gather x1, blocking collectives, per_device(): tests = lax.all_gather(sketch, COL, axis=0, tiled=True)  43 us
    all_gather x1, waiting for transfers between devices, per_device(): points = lax.all_gather(embeddings, COL, axis=0, tiled=True)  32.5 us
    dot_general x8, matrix products, step(): jnp.dot(tile, block_tests, preferred_element_type=jnp.float32)  16.7 us
    all_to_all x1, blocking collectives, sent_and_summed(): lax.all_to_all(in_blocks(shard, dim, length), axis, 0, 0, tiled=True)  14.7 us
    all_to_all x2, starting transfers between devices, from_everyone(): return lax.all_to_all(copies, axis, split_axis=0, concat_axis=0, tiled=True)  13 us
    reduce_sum x9, other arithmetic, squares_of(): return jnp.sum(jnp.square(points.astype(jnp.float32)), axis=1)  10 us
    another operation x3, other arithmetic, per_device(): lower_two = jnp.linalg.cholesky(gram_two)  6.52 us
  transfers between devices with their start and end apart: 3, of which 2 were waited for; matrix products, arithmetic and copies ran while one was open for 1% of the time, Pallas kernels for 0%

commit v1 on v0

v1 whole, which is shorter than its diff:
```python
import functools
import math

import jax
import jax.numpy as jnp
from jax import lax
from jax.experimental import pallas as pl
from jax.experimental.pallas import tpu as pltpu
from jax.sharding import Mesh
from jax.sharding import PartitionSpec as P

MESH = pl.DeviceIdType.MESH
AXES = ("x", "core", "y", "z")
NX, NY, NZ = 4, 4, 8
PTS, WIDTH, RANK = 128, 512, 64
PLANE = [
    (0, 0),
    (1, 0), (3, 0), (0, 1), (0, 3),
    (1, 1), (3, 1), (1, 3), (3, 3), (2, 0), (0, 2),
    (2, 1), (2, 3), (1, 2), (3, 2),
    (2, 2),
]
LINE = [0, 1, 7, 2, 6, 3, 5, 4]
PLANE_AT = {offset: at for at, offset in enumerate(PLANE)}
LINE_AT = {offset: at for at, offset in enumerate(LINE)}
N_COPIES = 96
PART = jnp.float32


def high_dot(left, right, dims):
    return lax.dot_general(
        left, right, (dims, ((), ())),
        precision=lax.Precision.HIGHEST,
        preferred_element_type=jnp.float32,
    )


def side_by_side(block):
    half = block.shape[0] // 2
    return jnp.concatenate([block[:half], block[half:]], axis=1)


def one_above_other(block):
    half = block.shape[1] // 2
    return jnp.concatenate([block[:, :half], block[:, half:]], axis=0)


def inverse_of_cholesky(sym):
    n = sym.shape[0]
    sub = lax.broadcasted_iota(jnp.int32, (n, n), 0)
    lane = lax.broadcasted_iota(jnp.int32, (n, n), 1)
    work = jnp.concatenate([sym, (sub == lane).astype(jnp.float32)], axis=1)
    tile = 8
    in_tile = lax.broadcasted_iota(jnp.int32, (tile, 2 * n), 0)
    tiles = [work[t * tile : (t + 1) * tile] for t in range(n // tile)]
    for p in range(n // tile):
        base = p * tile
        rows = tiles[p]
        below = list(range(p, n // tile))
        cols = [
            [jnp.broadcast_to(tiles[t][:, base + k : base + k + 1], (tile, 2 * n)) for t in below]
            for k in range(tile)
        ]
        done = []
        for k in range(tile):
            inv = lax.rsqrt(jnp.broadcast_to(cols[k][0][k : k + 1], (tile, 2 * n)))
            low = [c * inv for c in cols[k]]
            row = jnp.broadcast_to(rows[k : k + 1], (tile, 2 * n)) * inv
            for m in range(k + 1, tile):
                scale = jnp.broadcast_to(low[0][m : m + 1], (tile, 2 * n))
                cols[m] = [c - l * scale for c, l in zip(cols[m], low)]
            rows = jnp.where(in_tile > k, rows - low[0] * row, jnp.where(in_tile == k, row, rows))
            done.append((low, row))
        tiles[p] = rows
        for t in range(p + 1, n // tile):
            acc = tiles[t]
            for low, row in done:
                acc = acc - low[t - p] * row
            tiles[t] = acc
    return jnp.concatenate(tiles, axis=0)[:, n:]


def kernel(
    e_hbm, s_ref, basis_ref, first_ref,
    ea, eb, sd, naf, nbf, y_acc, rs_out, rs_in, gram, g_part, g_x, g_y, g_z, g_sum, inv_pair,
    load_sem, send_sem, recv_sem,
):
    me = {axis: lax.axis_index(axis) for axis in AXES}
    core = me["core"]
    coef = 3.0 / WIDTH * math.log2(math.e)

    def shift(axis, by, size):
        return lax.rem(me[axis] + by, size)

    def plane_peer(dx, dy):
        return {"x": shift("x", dx, NX), "y": shift("y", dy, NY)}

    partner = {"core": 1 - core}
    left, right = plane_peer(NX - 1, 0), plane_peer(1, 0)
    down, up = plane_peer(0, NY - 1), plane_peer(0, 1)
    below, above = {"z": shift("z", NZ - 1, NZ)}, {"z": shift("z", 1, NZ)}

    copies = {}

    def send(key, src, dst, to):
        at = len(copies)
        copy = pltpu.make_async_remote_copy(
            src_ref=src, dst_ref=dst,
            send_sem=send_sem.at[at], recv_sem=recv_sem.at[at],
            device_id=to, device_id_type=MESH,
        )
        copy.start()
        assert key not in copies
        copies[key] = copy

    def arrived(*keys):
        for key in keys:
            copies[key].wait_recv()

    own_a = pltpu.make_async_copy(e_hbm, ea.at[0, pl.ds(0, PTS)], load_sem.at[0])
    own_b = pltpu.make_async_copy(e_hbm, eb.at[pl.ds(0, PTS)], load_sem.at[1])
    own_b.start()
    own_a.start()

    barrier = pltpu.get_barrier_semaphore()
    peers = [partner]
    peers += [plane_peer(dx, dy) for dx, dy in PLANE[1:]]
    peers += [{"z": shift("z", dz, NZ)} for dz in range(1, NZ)]
    for peer in peers:
        pl.semaphore_signal(barrier, inc=1, device_id=peer, device_id_type=MESH)

    own_b.wait()
    own_a.wait()
    points = eb[0:PTS].astype(jnp.float32)
    norms = high_dot(jnp.ones((16, WIDTH), jnp.float32), points * points, ((1,), (1,)))
    one = norms.astype(jnp.bfloat16).astype(jnp.float32)
    two = (norms - one).astype(jnp.bfloat16).astype(jnp.float32)
    three = norms - one - two
    at_row = lax.broadcasted_iota(jnp.int32, norms.shape, 0)
    split = jnp.where(at_row == 0, one, jnp.where(at_row == 1, two, three))
    sd[0, 0:RANK, 0:PTS] = s_ref[...].astype(jnp.float32).T.astype(jnp.bfloat16)
    sd[0, RANK : RANK + 16, 0:PTS] = split.astype(jnp.bfloat16)
    pl.semaphore_wait(barrier, len(peers))

    def send_plane(offset, rows, to, by):
        dx, dy = offset
        there = ((dx + by[0]) % NX, (dy + by[1]) % NY)
        lo, hi = rows
        send(
            (there, lo),
            eb.at[pl.ds(PLANE_AT[offset] * PTS + lo, hi - lo)],
            eb.at[pl.ds(PLANE_AT[there] * PTS + lo, hi - lo)],
            to,
        )

    def to_left(offset, lo, hi):
        send_plane(offset, (lo, hi), left, (1, 0))

    def to_right(offset, lo, hi):
        send_plane(offset, (lo, hi), right, (-1, 0))

    def to_down(offset, lo, hi):
        send_plane(offset, (lo, hi), down, (0, 1))

    def to_up(offset, lo, hi):
        send_plane(offset, (lo, hi), up, (0, -1))

    def send_line(offset, lo, hi, to, by, side):
        there = (offset + by) % NZ
        a, b = LINE_AT[offset], LINE_AT[there]
        if side:
            send(("side", there), sd.at[a, :, pl.ds(0, PTS)], sd.at[b, :, pl.ds(0, PTS)], to)
        send(("line", there, lo), ea.at[a, pl.ds(lo, hi - lo)], ea.at[b, pl.ds(lo, hi - lo)], to)

    def send_partner(offset):
        a = LINE_AT[offset]
        send(("pside", offset), sd.at[a, :, pl.ds(0, PTS)], sd.at[a, :, pl.ds(PTS, PTS)], partner)
        send(("pline", offset), ea.at[a, pl.ds(0, PTS)], ea.at[a, pl.ds(PTS, PTS)], partner)

    def norms_of_line(offset):
        arrived(("pside", offset), ("pline", offset))
        a = LINE_AT[offset]
        parts = sd[a, RANK : RANK + 16, :].astype(jnp.float32)
        total = (parts[0:1] + parts[1:2]) + parts[2:3]
        naf[a] = jnp.broadcast_to(total * coef, (8, 2 * PTS))

    def norms_of_plane(lo, hi):
        for at in range(lo, hi):
            block = eb[at * PTS : (at + 1) * PTS].astype(jnp.float32)
            total = jnp.sum(block * block, axis=1, keepdims=True) * coef
            nbf[at * PTS : (at + 1) * PTS] = jnp.broadcast_to(total, (PTS, 128))

    def multiply(lines, lo, hi, first=False):
        at = lo
        while at < hi:
            blocks = min(4, hi - at)
            rows = slice(at * PTS, (at + blocks) * PTS)
            total = None
            for a in lines:
                cross = lax.dot_general(
                    eb[rows], ea[a], (((1,), (1,)), ((), ())), preferred_element_type=jnp.float32
                )
                side = jnp.concatenate([nbf[rows], nbf[rows]], axis=1)
                tile = jnp.exp2(cross * (2.0 * coef) - naf[a, 0:1] - side).astype(jnp.bfloat16)
                term = lax.dot_general(
                    tile, sd[a, 0:RANK], (((1,), (1,)), ((), ())), preferred_element_type=jnp.float32
                )
                total = term if total is None else total + term
            y_acc[rows] = total if first else y_acc[rows] + total
            at += blocks

    own = (0, 0)
    to_left(own, 0, PTS)
    to_right(own, 0, PTS)
    to_down(own, 0, PTS)
    to_up(own, 0, PTS)
    send_line(0, 0, PTS, below, 1, True)
    send_line(0, 0, PTS, above, -1, True)
    send_partner(0)
    norms_of_plane(0, 1)
    norms_of_line(0)

    arrived(("side", 1), ("line", 1, 0))
    send_line(1, 0, PTS, below, 1, True)
    send_partner(1)
    arrived(("side", 7), ("line", 7, 0))
    send_line(7, 0, PTS, above, -1, True)
    send_partner(7)
    arrived(((1, 0), 0))
    to_down((1, 0), 0, 64)
    to_up((1, 0), 0, 64)
    to_left((1, 0), 0, 32)
    arrived(((3, 0), 0))
    to_down((3, 0), 0, 64)
    to_up((3, 0), 0, 64)
    to_right((3, 0), 32, 64)
    arrived(((0, 1), 0))
    to_left((0, 1), 64, 128)
    to_right((0, 1), 64, 128)
    to_down((0, 1), 64, 96)
    arrived(((0, 3), 0))
    to_left((0, 3), 64, 128)
    to_right((0, 3), 64, 128)
    to_up((0, 3), 96, 128)
    to_left((1, 0), 64, 128)
    to_down((0, 1), 0, 64)
    norms_of_plane(1, 5)
    multiply([0], 0, 5, first=True)
    norms_of_line(1)
    norms_of_line(7)
    multiply([1, 2], 0, 5)

    arrived(("side", 2), ("line", 2, 0))
    send_line(2, 0, PTS, below, 1, True)
    send_partner(2)
    arrived(("side", 6), ("line", 6, 0))
    send_line(6, 0, PTS, above, -1, True)
    send_partner(6)
    arrived(((2, 0), 0), ((2, 0), 32))
    to_down((2, 0), 0, 64)
    to_up((2, 0), 0, 64)
    arrived(((0, 2), 64), ((0, 2), 96))
    to_left((0, 2), 64, 128)
    to_right((0, 2), 64, 128)
    arrived(((1, 1), 0))
    to_down((1, 1), 0, 64)
    arrived(((3, 3), 0))
    to_up((3, 3), 0, 64)
    arrived(((1, 1), 64))
    to_left((1, 1), 64, 128)
    arrived(((3, 3), 64))
    to_right((3, 3), 64, 128)
    arrived(((3, 1), 0), ((3, 1), 64), ((1, 3), 0), ((1, 3), 64), ((2, 0), 64), ((0, 2), 0))
    norms_of_plane(5, 11)
    multiply([0, 1, 2], 5, 11, first=True)
    norms_of_line(2)
    norms_of_line(6)
    multiply([3, 4], 0, 11)

    arrived(("side", 3), ("line", 3, 0))
    send_line(3, 0, 64, below, 1, True)
    send_partner(3)
    arrived(("side", 5), ("line", 5, 0))
    send_line(5, 64, 128, above, -1, False)
    send_partner(5)
    arrived(((2, 3), 0))
    to_up((2, 3), 0, 64)
    arrived(((3, 2), 64))
    to_right((3, 2), 64, 128)
    arrived(((2, 1), 0), ((2, 1), 64), ((2, 3), 64), ((1, 2), 0), ((1, 2), 64), ((3, 2), 0))
    norms_of_plane(11, 15)
    multiply([0, 1, 2, 3, 4], 11, 15, first=True)
    arrived(("side", 4), ("line", 4, 0), ("line", 4, 64))
    send_partner(4)
    norms_of_line(3)
    norms_of_line(5)
    multiply([5, 6], 0, 15)

    arrived(((2, 2), 0), ((2, 2), 64))
    norms_of_plane(15, 16)
    multiply([0, 1, 2, 3, 4, 5, 6], 15, 16, first=True)
    norms_of_line(4)
    for lo in range(0, 16, 4):
        multiply([7], lo, lo + 4)
        for at in range(lo, lo + 4):
            rs_out[at] = side_by_side(y_acc[at * PTS : (at + 1) * PTS]).astype(PART)
        for at in range(max(lo, 1), lo + 4):
            dx, dy = PLANE[at]
            there = PLANE_AT[(-dx % NX, -dy % NY)]
            send(("part", there), rs_out.at[at], rs_in.at[there], plane_peer(dx, dy))

    total = side_by_side(y_acc[0:PTS])
    for at in range(1, 16):
        arrived(("part", at))
        total = total + rs_in[at].astype(jnp.float32)
    sketched = one_above_other(total)
    tests = s_ref[...].astype(jnp.float32)
    products = high_dot(
        jnp.concatenate([tests, sketched], axis=1),
        jnp.concatenate([sketched, tests], axis=1),
        ((0,), (0,)),
    )
    gram[0] = side_by_side(0.5 * (products[:RANK, :RANK] + products[RANK:, RANK:]))
    gram[1] = side_by_side(products[RANK:, :RANK])

    send("core", gram.at[1 - core], g_part, partner)
    arrived("core")
    g_sum[0] = gram[core] + g_part[...]
    for stage, axis, size, landing in ((0, "x", NX, g_x), (1, "y", NY, g_y), (2, "z", NZ, g_z)):
        for by in range(1, size):
            send((axis, by), g_sum.at[stage], landing.at[by - 1], {axis: shift(axis, by, size)})
        value = g_sum[stage]
        for by in range(1, size):
            arrived((axis, by))
            value = value + landing[by - 1]
        if stage < 2:
            g_sum[stage + 1] = value
    mine = one_above_other(value)
    inv = inverse_of_cholesky(mine)
    inv_pair[core] = side_by_side(inv)
    send("inv", inv_pair.at[core], inv_pair.at[core], partner)
    arrived("inv")
    scale = math.sqrt(PTS * 256)
    low = one_above_other(inv_pair[0])
    low_two = one_above_other(inv_pair[1])
    first_ref[...] = high_dot(sketched, low, ((1,), (1,))) * scale
    basis_ref[...] = high_dot(sketched, low_two, ((1,), (1,))) * scale
    for copy in copies.values():
        copy.wait_send()
    assert len(copies) <= N_COPIES


def per_device(embeddings, sketch):
    vmem = pl.BlockSpec(memory_space=pltpu.VMEM)
    out = jax.ShapeDtypeStruct((PTS, RANK), jnp.float32)
    packed = (RANK // 2, 2 * RANK)
    basis, first = pl.pallas_call(
        kernel,
        out_shape=(out, out),
        in_specs=[pl.BlockSpec(memory_space=pl.ANY), vmem],
        out_specs=(vmem, vmem),
        scratch_shapes=[
            pltpu.VMEM((NZ, 2 * PTS, WIDTH), jnp.bfloat16),
            pltpu.VMEM((16 * PTS, WIDTH), jnp.bfloat16),
            pltpu.VMEM((NZ, RANK + 16, 2 * PTS), jnp.bfloat16),
            pltpu.VMEM((NZ, 8, 2 * PTS), jnp.float32),
            pltpu.VMEM((16 * PTS, 128), jnp.float32),
            pltpu.VMEM((16 * PTS, RANK), jnp.float32),
            pltpu.VMEM((16, PTS // 2, 2 * RANK), PART),
            pltpu.VMEM((16, PTS // 2, 2 * RANK), PART),
            pltpu.VMEM((2, *packed), jnp.float32),
            pltpu.VMEM(packed, jnp.float32),
            pltpu.VMEM((NX - 1, *packed), jnp.float32),
            pltpu.VMEM((NY - 1, *packed), jnp.float32),
            pltpu.VMEM((NZ - 1, *packed), jnp.float32),
            pltpu.VMEM((3, *packed), jnp.float32),
            pltpu.VMEM((2, *packed), jnp.float32),
            pltpu.SemaphoreType.DMA((2,)),
            pltpu.SemaphoreType.DMA((N_COPIES,)),
            pltpu.SemaphoreType.DMA((N_COPIES,)),
        ],
        compiler_params=pltpu.CompilerParams(
            collective_id=0, has_side_effects=True, vmem_limit_bytes=40 << 20
        ),
        name="nystrom",
    )(embeddings, sketch)
    return basis, first


def solution(mesh):
    torus = Mesh(mesh.devices.reshape(NX, 2, NY, NZ), AXES)
    spec = P(AXES, None)
    return jax.shard_map(
        per_device, mesh=torus, in_specs=(spec, spec), out_specs=(spec, spec), check_vma=False
    )
```

time: 240 us -> 65.4 us (0.27)
  blocking collectives: 108 us -> 0 us
  Pallas kernels: 0 us -> 61.5 us
  other arithmetic: 40.7 us -> 0 us
  waiting for transfers between devices: 37.8 us -> 0 us
  matrix products: 18.2 us -> 0 us
  between operations: 14.3 us -> 0.65 us
  starting transfers between devices: 13.1 us -> 0 us
  local copies, waits for them, and re-layouts: 6.8 us -> 3.13 us
    all_to_all x4 -> x0, blocking collectives: 64.7 us -> none  [the longest x3 50 us: from_everyone(): return lax.all_to_all(copies, axis, split_axis=0, concat_axis=0, tiled=True)]
    pallas_call x0 -> x1, Pallas kernels: none -> 61.5 us  [per_device(): pl.pallas_call(kernel, out_shape=(out, out), in_specs=[pl.BlockSpec(memor...]
    all_gather x1 -> x0, blocking collectives: 43 us -> none  [per_device(): tests = lax.all_gather(sketch, COL, axis=0, tiled=True)]
    all_gather x1 -> x0, waiting for transfers between devices: 32.5 us -> none  [per_device(): points = lax.all_gather(embeddings, COL, axis=0, tiled=True)]
    another operation x10 -> x0, other arithmetic: 24.1 us -> none  [the longest x3 6.52 us: per_device(): lower_two = jnp.linalg.cholesky(gram_two)]
    dot_general x10 -> x0, matrix products: 17 us -> none  [the longest x8 16.7 us: step(): jnp.dot(tile, block_tests, preferred_element_type=jnp.float32)]
    all_to_all x2 -> x0, starting transfers between devices: 13 us -> none  [from_everyone(): return lax.all_to_all(copies, axis, split_axis=0, concat_axis=0, tiled=True)]
    reduce_sum x14 -> x0, other arithmetic: 10.3 us -> none  [the longest x9 10 us: squares_of(): return jnp.sum(jnp.square(points.astype(jnp.float32)), axis=1)]
  transfers between devices with their start and end apart: 3 -> 0, of which waited for: 2 -> 0; matrix products, arithmetic and copies ran while one was open for 1% -> 0% of each run, Pallas kernels for 0% -> 0%
where the time goes in v1:
time: 65.4 us; the launch traced here: 65.2 us
  Pallas kernels  61.5 us (94%)
  local copies, waits for them, and re-layouts  3.13 us (5%)
    pallas_call x1, Pallas kernels, per_device(): pl.pallas_call(kernel, out_shape=(out, out), in_specs=[pl.BlockSpec(memor...  61.5 us
    unnamed x3, local copies, waits for them, and re-layouts  1.73 us
    pallas_call x2, local copies, waits for them, and re-layouts, per_device(): pl.pallas_call(kernel, out_shape=(out, out), in_specs=[pl.BlockSpec(memor...  1.4 us

profile of v1, /device:TPU:1, one launch (start us, length us, event | category | flops | bytes accessed | tf_op | source)
XLA Modules:
  0.0 65.2 jit_solution(15056366708660600325)
XLA Ops:
  0.6 0.8 %copy.4.s_ref = bf16[128,64]{1,0:T(8,128)(2,1)S(1)} copy(bf16[128,64]{0,1:T(8,128)(2,1)} %param.3) | data formatting | bytes 32768 | tf_op args[1]
  1.5 0.0 copy-start
  1.5 0.9 %copy-done = bf16[128,512]{1,0:T(8,128)(2,1)S(1)} copy-done((bf16[128,512]{1,0:T(8,128)(2,1)S(1)}, bf16[128,512]{1,0:T(8,128)(2,1)}, u32[]{:S(2)}) %copy-start) | copy-done | bytes 131096
  2.4 61.5 %nystrom.1 = (f32[128,64]{1,0:T(8,128)S(1)}, f32[128,64]{1,0:T(8,128)S(1)}) custom-call(bf16[128,512]{1,0:T(8,128)(2,1)S(1)} %copy-done, bf16[128,64]{1,0:T(8,128)(2,1)S(1)} %copy.4.s_ref), custom_call_target="tpu_custom_call" | custom-call | tf_op jit(solution)/shard_map/nystrom/pallas_call | solution.py:357
  63.8 0.7 %copy.5 = f32[128,64]{0,1:T(8,128)} copy(f32[128,64]{1,0:T(8,128)S(1)} %get-tuple-element.2) | data formatting | bytes 65536 | tf_op jit(solution)/shard_map/nystrom/pallas_call | solution.py:357
  64.5 0.7 %copy.6 = f32[128,64]{0,1:T(8,128)} copy(f32[128,64]{1,0:T(8,128)S(1)} %get-tuple-element.3) | data formatting | bytes 65536 | tf_op jit(solution)/shard_map/nystrom/pallas_call | solution.py:357
Async XLA Ops:
  1.5 0.9 %copy-start = (bf16[128,512]{1,0:T(8,128)(2,1)S(1)}, bf16[128,512]{1,0:T(8,128)(2,1)}, u32[]{:S(2)}) copy-start(bf16[128,512]{1,0:T(8,128)(2,1)} %e_hbm.1) | copy-start | bytes 393220

commit v2 on v1

--- a/solution.py
+++ b/solution.py
@@ -23,7 +23,7 @@
 LINE = [0, 1, 7, 2, 6, 3, 5, 4]
 PLANE_AT = {offset: at for at, offset in enumerate(PLANE)}
 LINE_AT = {offset: at for at, offset in enumerate(LINE)}
-N_COPIES = 96
+N_COPIES = 128
 PART = jnp.float32
 
 
@@ -81,8 +81,8 @@
 
 
 def kernel(
-    e_hbm, s_ref, basis_ref, first_ref,
-    ea, eb, sd, naf, nbf, y_acc, rs_out, rs_in, gram, g_part, g_x, g_y, g_z, g_sum, inv_pair,
+    e_hbm, s_hbm, both_ref,
+    ea, eb, sd, naf, nbf, y_acc, tests_ref, rs_out, rs_in, gram, g_part, g_x, g_y, g_z, g_sum, inv_pair,
     load_sem, send_sem, recv_sem,
 ):
     me = {axis: lax.axis_index(axis) for axis in AXES}
@@ -117,20 +117,19 @@
         for key in keys:
             copies[key].wait_recv()
 
-    own_a = pltpu.make_async_copy(e_hbm, ea.at[0, pl.ds(0, PTS)], load_sem.at[0])
-    own_b = pltpu.make_async_copy(e_hbm, eb.at[pl.ds(0, PTS)], load_sem.at[1])
-    own_b.start()
-    own_a.start()
-
+    loads = [
+        pltpu.make_async_copy(e_hbm, eb.at[pl.ds(0, PTS)], load_sem.at[0]),
+        pltpu.make_async_copy(s_hbm, sd.at[0, pl.ds(0, RANK), pl.ds(0, PTS)], load_sem.at[1]),
+        pltpu.make_async_copy(e_hbm, ea.at[0, pl.ds(0, PTS)], load_sem.at[2]),
+    ]
+    for load in loads:
+        load.start()
     barrier = pltpu.get_barrier_semaphore()
-    peers = [partner]
-    peers += [plane_peer(dx, dy) for dx, dy in PLANE[1:]]
-    peers += [{"z": shift("z", dz, NZ)} for dz in range(1, NZ)]
+    peers = [partner, left, right, down, up, below, above, plane_peer(2, 0), plane_peer(0, 2)]
     for peer in peers:
         pl.semaphore_signal(barrier, inc=1, device_id=peer, device_id_type=MESH)
-
-    own_b.wait()
-    own_a.wait()
+    for load in loads:
+        load.wait()
     points = eb[0:PTS].astype(jnp.float32)
     norms = high_dot(jnp.ones((16, WIDTH), jnp.float32), points * points, ((1,), (1,)))
     one = norms.astype(jnp.bfloat16).astype(jnp.float32)
@@ -138,8 +137,8 @@
     three = norms - one - two
     at_row = lax.broadcasted_iota(jnp.int32, norms.shape, 0)
     split = jnp.where(at_row == 0, one, jnp.where(at_row == 1, two, three))
-    sd[0, 0:RANK, 0:PTS] = s_ref[...].astype(jnp.float32).T.astype(jnp.bfloat16)
     sd[0, RANK : RANK + 16, 0:PTS] = split.astype(jnp.bfloat16)
+    tests_ref[...] = sd[0, 0:RANK, 0:PTS].astype(jnp.float32).T
     pl.semaphore_wait(barrier, len(peers))
 
     def send_plane(offset, rows, to, by):
@@ -209,59 +208,71 @@
             y_acc[rows] = total if first else y_acc[rows] + total
             at += blocks
 
+    def across(axis, lo, hi):
+        there, to = ((2, 0), plane_peer(2, 0)) if axis == "x" else ((0, 2), plane_peer(0, 2))
+        send_plane((0, 0), (lo, hi), to, there)
+
+    def line_on(offset, lo, hi, to, by, side=None):
+        arrived(*([("side", offset)] if lo == 0 else []), ("line", offset, lo))
+        send_line(offset, lo, hi, to, by, (lo == 0) if side is None else side)
+
     own = (0, 0)
-    to_left(own, 0, PTS)
-    to_right(own, 0, PTS)
-    to_down(own, 0, PTS)
-    to_up(own, 0, PTS)
-    send_line(0, 0, PTS, below, 1, True)
-    send_line(0, 0, PTS, above, -1, True)
+    send_line(0, 0, 64, below, 1, True)
+    send_line(0, 0, 64, above, -1, True)
+    to_left(own, 0, 64)
+    to_right(own, 0, 64)
+    to_down(own, 64, 128)
+    to_up(own, 64, 128)
+    across("x", 0, 64)
+    across("y", 64, 128)
+    send_line(0, 64, 128, below, 1, False)
+    send_line(0, 64, 128, above, -1, False)
+    to_left(own, 64, 128)
+    to_right(own, 64, 128)
+    to_down(own, 0, 64)
+    to_up(own, 0, 64)
     send_partner(0)
     norms_of_plane(0, 1)
     norms_of_line(0)
-
-    arrived(("side", 1), ("line", 1, 0))
-    send_line(1, 0, PTS, below, 1, True)
-    send_partner(1)
-    arrived(("side", 7), ("line", 7, 0))
-    send_line(7, 0, PTS, above, -1, True)
-    send_partner(7)
+    multiply([0], 0, 1, first=True)
+
+    line_on(1, 0, 64, below, 1)
+    line_on(7, 0, 64, above, -1)
     arrived(((1, 0), 0))
     to_down((1, 0), 0, 64)
     to_up((1, 0), 0, 64)
-    to_left((1, 0), 0, 32)
     arrived(((3, 0), 0))
     to_down((3, 0), 0, 64)
     to_up((3, 0), 0, 64)
-    to_right((3, 0), 32, 64)
-    arrived(((0, 1), 0))
+    arrived(((0, 1), 64))
     to_left((0, 1), 64, 128)
     to_right((0, 1), 64, 128)
-    to_down((0, 1), 64, 96)
-    arrived(((0, 3), 0))
+    arrived(((0, 3), 64))
     to_left((0, 3), 64, 128)
     to_right((0, 3), 64, 128)
-    to_up((0, 3), 96, 128)
+    line_on(1, 64, 128, below, 1)
+    send_partner(1)
+    line_on(7, 64, 128, above, -1)
+    send_partner(7)
+    arrived(((2, 0), 0))
+    to_down((2, 0), 0, 64)
+    to_up((2, 0), 0, 64)
+    arrived(((0, 2), 64))
+    to_left((0, 2), 64, 128)
+    to_right((0, 2), 64, 128)
+    arrived(((1, 0), 64))
     to_left((1, 0), 64, 128)
+    arrived(((0, 1), 0))
     to_down((0, 1), 0, 64)
+    arrived(((3, 0), 64), ((0, 3), 0))
     norms_of_plane(1, 5)
-    multiply([0], 0, 5, first=True)
+    multiply([0], 1, 5, first=True)
     norms_of_line(1)
     norms_of_line(7)
     multiply([1, 2], 0, 5)
 
-    arrived(("side", 2), ("line", 2, 0))
-    send_line(2, 0, PTS, below, 1, True)
-    send_partner(2)
-    arrived(("side", 6), ("line", 6, 0))
-    send_line(6, 0, PTS, above, -1, True)
-    send_partner(6)
-    arrived(((2, 0), 0), ((2, 0), 32))
-    to_down((2, 0), 0, 64)
-    to_up((2, 0), 0, 64)
-    arrived(((0, 2), 64), ((0, 2), 96))
-    to_left((0, 2), 64, 128)
-    to_right((0, 2), 64, 128)
+    line_on(2, 0, 64, below, 1)
+    line_on(6, 0, 64, above, -1)
     arrived(((1, 1), 0))
     to_down((1, 1), 0, 64)
     arrived(((3, 3), 0))
@@ -270,6 +281,14 @@
     to_left((1, 1), 64, 128)
     arrived(((3, 3), 64))
     to_right((3, 3), 64, 128)
+    line_on(2, 64, 128, below, 1)
+    send_partner(2)
+    line_on(6, 64, 128, above, -1)
+    send_partner(6)
+    arrived(((2, 3), 0))
+    to_up((2, 3), 0, 64)
+    arrived(((3, 2), 64))
+    to_right((3, 2), 64, 128)
     arrived(((3, 1), 0), ((3, 1), 64), ((1, 3), 0), ((1, 3), 64), ((2, 0), 64), ((0, 2), 0))
     norms_of_plane(5, 11)
     multiply([0, 1, 2], 5, 11, first=True)
@@ -277,34 +296,28 @@
     norms_of_line(6)
     multiply([3, 4], 0, 11)
 
-    arrived(("side", 3), ("line", 3, 0))
-    send_line(3, 0, 64, below, 1, True)
-    send_partner(3)
-    arrived(("side", 5), ("line", 5, 0))
+    line_on(3, 0, 64, below, 1)
+    arrived(("side", 5), ("line", 5, 0), ("line", 5, 64))
     send_line(5, 64, 128, above, -1, False)
     send_partner(5)
-    arrived(((2, 3), 0))
-    to_up((2, 3), 0, 64)
-    arrived(((3, 2), 64))
-    to_right((3, 2), 64, 128)
-    arrived(((2, 1), 0), ((2, 1), 64), ((2, 3), 64), ((1, 2), 0), ((1, 2), 64), ((3, 2), 0))
-    norms_of_plane(11, 15)
-    multiply([0, 1, 2, 3, 4], 11, 15, first=True)
+    arrived(("line", 3, 64))
+    send_partner(3)
+    arrived(((2, 1), 0), ((2, 1), 64), ((2, 3), 64), ((1, 2), 0), ((1, 2), 64), ((3, 2), 0), ((2, 2), 0), ((2, 2), 64))
+    norms_of_plane(11, 16)
+    multiply([0, 1, 2, 3, 4], 11, 16, first=True)
+    norms_of_line(3)
+    norms_of_line(5)
+    multiply([5, 6], 8, 16)
     arrived(("side", 4), ("line", 4, 0), ("line", 4, 64))
     send_partner(4)
-    norms_of_line(3)
-    norms_of_line(5)
-    multiply([5, 6], 0, 15)
-
-    arrived(((2, 2), 0), ((2, 2), 64))
-    norms_of_plane(15, 16)
-    multiply([0, 1, 2, 3, 4, 5, 6], 15, 16, first=True)
+    multiply([5, 6], 0, 8)
+
     norms_of_line(4)
-    for lo in range(0, 16, 4):
+    for lo in (12, 8, 4, 0):
         multiply([7], lo, lo + 4)
-        for at in range(lo, lo + 4):
+        for at in reversed(range(max(lo, 1), lo + 4)):
             rs_out[at] = side_by_side(y_acc[at * PTS : (at + 1) * PTS]).astype(PART)
-        for at in range(max(lo, 1), lo + 4):
+        for at in reversed(range(max(lo, 1), lo + 4)):
             dx, dy = PLANE[at]
             there = PLANE_AT[(-dx % NX, -dy % NY)]
             send(("part", there), rs_out.at[at], rs_in.at[there], plane_peer(dx, dy))
@@ -314,7 +327,7 @@
         arrived(("part", at))
         total = total + rs_in[at].astype(jnp.float32)
     sketched = one_above_other(total)
-    tests = s_ref[...].astype(jnp.float32)
+    tests = tests_ref[...]
     products = high_dot(
         jnp.concatenate([tests, sketched], axis=1),
         jnp.concatenate([sketched, tests], axis=1),
@@ -343,8 +356,7 @@
     scale = math.sqrt(PTS * 256)
     low = one_above_other(inv_pair[0])
     low_two = one_above_other(inv_pair[1])
-    first_ref[...] = high_dot(sketched, low, ((1,), (1,))) * scale
-    basis_ref[...] = high_dot(sketched, low_two, ((1,), (1,))) * scale
+    both_ref[...] = high_dot(jnp.concatenate([low_two, low], axis=0), sketched, ((1,), (1,))) * scale
     for copy in copies.values():
         copy.wait_send()
     assert len(copies) <= N_COPIES
@@ -352,13 +364,12 @@
 
 def per_device(embeddings, sketch):
     vmem = pl.BlockSpec(memory_space=pltpu.VMEM)
-    out = jax.ShapeDtypeStruct((PTS, RANK), jnp.float32)
     packed = (RANK // 2, 2 * RANK)
-    basis, first = pl.pallas_call(
+    both = pl.pallas_call(
         kernel,
-        out_shape=(out, out),
-        in_specs=[pl.BlockSpec(memory_space=pl.ANY), vmem],
-        out_specs=(vmem, vmem),
+        out_shape=jax.ShapeDtypeStruct((2 * RANK, PTS), jnp.float32),
+        in_specs=[pl.BlockSpec(memory_space=pl.ANY)] * 2,
+        out_specs=vmem,
         scratch_shapes=[
             pltpu.VMEM((NZ, 2 * PTS, WIDTH), jnp.bfloat16),
             pltpu.VMEM((16 * PTS, WIDTH), jnp.bfloat16),
@@ -366,6 +377,7 @@
             pltpu.VMEM((NZ, 8, 2 * PTS), jnp.float32),
             pltpu.VMEM((16 * PTS, 128), jnp.float32),
             pltpu.VMEM((16 * PTS, RANK), jnp.float32),
+            pltpu.VMEM((PTS, RANK), jnp.float32),
             pltpu.VMEM((16, PTS // 2, 2 * RANK), PART),
             pltpu.VMEM((16, PTS // 2, 2 * RANK), PART),
             pltpu.VMEM((2, *packed), jnp.float32),
@@ -375,16 +387,16 @@
             pltpu.VMEM((NZ - 1, *packed), jnp.float32),
             pltpu.VMEM((3, *packed), jnp.float32),
             pltpu.VMEM((2, *packed), jnp.float32),
-            pltpu.SemaphoreType.DMA((2,)),
+            pltpu.SemaphoreType.DMA((3,)),
             pltpu.SemaphoreType.DMA((N_COPIES,)),
             pltpu.SemaphoreType.DMA((N_COPIES,)),
         ],
         compiler_params=pltpu.CompilerParams(
-            collective_id=0, has_side_effects=True, vmem_limit_bytes=40 << 20
+            collective_id=0, has_side_effects=True, vmem_limit_bytes=67043328
         ),
         name="nystrom",
-    )(embeddings, sketch)
-    return basis, first
+    )(embeddings, sketch.T)
+    return both[:RANK].T, both[RANK:].T
 
 
 def solution(mesh):

time: 65.4 us -> 61.9 us (0.946)
  Pallas kernels: 61.5 us -> 59.6 us
  local copies, waits for them, and re-layouts: 3.13 us -> 1.4 us
    pallas_call x1, Pallas kernels: 61.5 us -> 59.6 us  [per_device(): pl.pallas_call(kernel, out_shape=jax.ShapeDtypeStruct((2 * RANK, PTS), jn...]
    unnamed x3 -> x0, local copies, waits for them, and re-layouts: 1.73 us -> none
    transpose x0 -> x1, local copies, waits for them, and re-layouts: none -> 1.4 us  [per_device(): return (both[:RANK].T, both[RANK:].T)]
    pallas_call x2 -> x0, local copies, waits for them, and re-layouts: 1.4 us -> none  [per_device(): pl.pallas_call(kernel, out_shape=(out, out), in_specs=[pl.BlockSpec(memor...]
where the time goes in v2:
time: 61.9 us; the launch traced here: 61.7 us
  Pallas kernels  59.6 us (96%)
  local copies, waits for them, and re-layouts  1.4 us (2%)
  between operations  0.64 us (1%)
    pallas_call x1, Pallas kernels, per_device(): pl.pallas_call(kernel, out_shape=jax.ShapeDtypeStruct((2 * RANK, PTS), jn...  59.6 us
    transpose x1, local copies, waits for them, and re-layouts, per_device(): return (both[:RANK].T, both[RANK:].T)  1.4 us

profile of v2, /device:TPU:1, one launch (start us, length us, event | category | flops | bytes accessed | tf_op | source)
XLA Modules:
  0.0 61.7 jit_solution(14986530682524024045)
XLA Ops:
  0.6 59.6 %nystrom.1 = f32[128,128]{1,0:T(8,128)} custom-call(bf16[128,512]{1,0:T(8,128)(2,1)} %e_hbm.1, bf16[64,128]{1,0:T(8,128)(2,1)} %bitcast.5), custom_call_target="tpu_custom_call" | custom-call | tf_op jit(solution)/shard_map/nystrom/pallas_call | solution.py:368
  60.3 1.4 %slice_bitcast_fusion = (f32[128,64]{0,1:T(8,128)}, f32[128,64]{0,1:T(8,128)}) fusion(f32[128,128]{1,0:T(8,128)} %nystrom.1), kind=kLoop, calls=%fused_computation | loop fusion | bytes 131072 | tf_op jit(solution)/shard_map/transpose | solution.py:399

commit v3 on v2

v3 whole, which is shorter than its diff:
```python
import functools
import math

import jax
import jax.numpy as jnp
from jax import lax
from jax.experimental import pallas as pl
from jax.experimental.pallas import tpu as pltpu
from jax.sharding import Mesh
from jax.sharding import PartitionSpec as P

MESH = pl.DeviceIdType.MESH
AXES = ("x", "core", "y", "z")
NX, NY, NZ = 4, 4, 8
PTS, WIDTH, RANK = 128, 512, 64
PLANE = [
    (0, 0),
    (1, 0), (3, 0), (0, 1), (0, 3),
    (1, 1), (3, 1), (1, 3), (3, 3), (2, 0), (0, 2),
    (2, 1), (2, 3), (1, 2), (3, 2),
    (2, 2),
]
LINE = [0, 1, 7, 2, 6, 3, 5, 4]
PLANE_AT = {offset: at for at, offset in enumerate(PLANE)}
LINE_AT = {offset: at for at, offset in enumerate(LINE)}
N_COPIES = 128
PART = jnp.float32


def high_dot(left, right, dims):
    return lax.dot_general(
        left, right, (dims, ((), ())),
        precision=lax.Precision.HIGHEST,
        preferred_element_type=jnp.float32,
    )


def side_by_side(block):
    half = block.shape[0] // 2
    return jnp.concatenate([block[:half], block[half:]], axis=1)


def one_above_other(block):
    half = block.shape[1] // 2
    return jnp.concatenate([block[:, :half], block[:, half:]], axis=0)


def inverses_of_cholesky(matrices):
    n = matrices[0].shape[0]
    sub = lax.broadcasted_iota(jnp.int32, (n, n), 0)
    lane = lax.broadcasted_iota(jnp.int32, (n, n), 1)
    unit = (sub == lane).astype(jnp.float32)
    tile = 8
    count = n // tile
    in_tile = lax.broadcasted_iota(jnp.int32, (tile, 2 * n), 0)
    every = range(len(matrices))
    tiles = []
    for matrix in matrices:
        work = jnp.concatenate([matrix, unit], axis=1)
        tiles.append([work[t * tile : (t + 1) * tile] for t in range(count)])
    for p in range(count):
        base = p * tile
        rows = [tiles[i][p] for i in every]
        cols = [
            [
                [jnp.broadcast_to(tiles[i][t][:, base + k : base + k + 1], (tile, 2 * n)) for t in range(p, count)]
                for k in range(tile)
            ]
            for i in every
        ]
        done = [[] for _ in every]
        for k in range(tile):
            inv = [lax.rsqrt(jnp.broadcast_to(cols[i][k][0][k : k + 1], (tile, 2 * n))) for i in every]
            low = [[c * inv[i] for c in cols[i][k]] for i in every]
            row = [jnp.broadcast_to(rows[i][k : k + 1], (tile, 2 * n)) * inv[i] for i in every]
            for m in range(k + 1, tile):
                for i in every:
                    scale = jnp.broadcast_to(low[i][0][m : m + 1], (tile, 2 * n))
                    cols[i][m] = [c - l * scale for c, l in zip(cols[i][m], low[i])]
            for i in every:
                rows[i] = jnp.where(
                    in_tile > k, rows[i] - low[i][0] * row[i], jnp.where(in_tile == k, row[i], rows[i])
                )
                done[i].append((low[i], row[i]))
        for t in range(p + 1, count):
            for i in every:
                acc = tiles[i][t]
                for low, row in done[i]:
                    acc = acc - low[t - p] * row
                tiles[i][t] = acc
        for i in every:
            tiles[i][p] = rows[i]
    return [jnp.concatenate(tiles[i], axis=0)[:, n:] for i in every]


def kernel(
    e_ref, s_ref, both_ref,
    ea, eb, sd, naf, nbf, y_acc, tests_ref, rs_out, rs_in, gram, g_part, g_x, g_y, g_z, g_sum,
    send_sem, recv_sem,
):
    me = {axis: lax.axis_index(axis) for axis in AXES}
    core = me["core"]
    coef = 3.0 / WIDTH * math.log2(math.e)

    def shift(axis, by, size):
        return lax.rem(me[axis] + by, size)

    def plane_peer(dx, dy):
        return {"x": shift("x", dx, NX), "y": shift("y", dy, NY)}

    partner = {"core": 1 - core}
    left, right = plane_peer(NX - 1, 0), plane_peer(1, 0)
    down, up = plane_peer(0, NY - 1), plane_peer(0, 1)
    below, above = {"z": shift("z", NZ - 1, NZ)}, {"z": shift("z", 1, NZ)}

    copies = {}

    def describe(key, src, dst, to):
        at = len(copies)
        assert key not in copies
        copies[key] = pltpu.make_async_remote_copy(
            src_ref=src, dst_ref=dst,
            send_sem=send_sem.at[at], recv_sem=recv_sem.at[at],
            device_id=to, device_id_type=MESH,
        )
        return copies[key]

    def send(key, src, dst, to):
        describe(key, src, dst, to).start()

    def arrived(*keys):
        for key in keys:
            copies[key].wait_recv()

    barrier = pltpu.get_barrier_semaphore()
    peers = [partner, left, right, down, up, below, above, plane_peer(2, 0), plane_peer(0, 2)]
    for peer in peers:
        pl.semaphore_signal(barrier, inc=1, device_id=peer, device_id_type=MESH)
    pl.semaphore_wait(barrier, len(peers))

    def send_plane(offset, rows, to, by):
        dx, dy = offset
        there = ((dx + by[0]) % NX, (dy + by[1]) % NY)
        lo, hi = rows
        source = e_ref if offset == (0, 0) else eb.at[pl.ds(PLANE_AT[offset] * PTS, PTS)]
        send(
            (there, lo),
            source.at[pl.ds(lo, hi - lo)],
            eb.at[pl.ds(PLANE_AT[there] * PTS + lo, hi - lo)],
            to,
        )

    def to_left(offset, lo, hi):
        send_plane(offset, (lo, hi), left, (1, 0))

    def to_right(offset, lo, hi):
        send_plane(offset, (lo, hi), right, (-1, 0))

    def to_down(offset, lo, hi):
        send_plane(offset, (lo, hi), down, (0, 1))

    def to_up(offset, lo, hi):
        send_plane(offset, (lo, hi), up, (0, -1))

    def send_line(offset, lo, hi, to, by):
        there = (offset + by) % NZ
        source = e_ref if offset == 0 else ea.at[LINE_AT[offset], pl.ds(0, PTS)]
        send(("line", there, lo), source.at[pl.ds(lo, hi - lo)], ea.at[LINE_AT[there], pl.ds(lo, hi - lo)], to)

    def send_side(offset, to, by):
        there = (offset + by) % NZ
        a, b = LINE_AT[offset], LINE_AT[there]
        send(("side", there), sd.at[a, :, pl.ds(0, PTS)], sd.at[b, :, pl.ds(0, PTS)], to)

    def send_partner(offset):
        a = LINE_AT[offset]
        source = e_ref if offset == 0 else ea.at[a, pl.ds(0, PTS)]
        send(("pline", offset), source, ea.at[a, pl.ds(PTS, PTS)], partner)

    def send_partner_side(offset):
        a = LINE_AT[offset]
        send(("pside", offset), sd.at[a, :, pl.ds(0, PTS)], sd.at[a, :, pl.ds(PTS, PTS)], partner)

    def norms_of_line(offset):
        arrived(("pside", offset), ("pline", offset))
        a = LINE_AT[offset]
        parts = sd[a, RANK : RANK + 16, :].astype(jnp.float32)
        total = (parts[0:1] + parts[1:2]) + parts[2:3]
        naf[a] = jnp.broadcast_to(total * coef, (8, 2 * PTS))

    def norms_of_plane(lo, hi):
        for at in range(lo, hi):
            block = eb[at * PTS : (at + 1) * PTS].astype(jnp.float32)
            total = jnp.sum(block * block, axis=1, keepdims=True) * coef
            nbf[at * PTS : (at + 1) * PTS] = jnp.broadcast_to(total, (PTS, 128))

    def multiply(lines, lo, hi, first=False):
        at = lo
        while at < hi:
            blocks = min(4, hi - at)
            rows = slice(at * PTS, (at + blocks) * PTS)
            total = None
            for a in lines:
                cross = lax.dot_general(
                    eb[rows], ea[a], (((1,), (1,)), ((), ())), preferred_element_type=jnp.float32
                )
                side = jnp.concatenate([nbf[rows], nbf[rows]], axis=1)
                tile = jnp.exp2(cross * (2.0 * coef) - naf[a, 0:1] - side).astype(jnp.bfloat16)
                term = lax.dot_general(
                    tile, sd[a, 0:RANK], (((1,), (1,)), ((), ())), preferred_element_type=jnp.float32
                )
                total = term if total is None else total + term
            y_acc[rows] = total if first else y_acc[rows] + total
            at += blocks

    def across(axis, lo, hi):
        there, to = ((2, 0), plane_peer(2, 0)) if axis == "x" else ((0, 2), plane_peer(0, 2))
        send_plane((0, 0), (lo, hi), to, there)

    def line_on(offset, lo, hi, to, by):
        arrived(("line", offset, lo))
        send_line(offset, lo, hi, to, by)

    def side_on(offset, to, by):
        arrived(("side", offset))
        send_side(offset, to, by)
        send_partner_side(offset)

    own = (0, 0)
    send_line(0, 0, 64, below, 1)
    send_line(0, 0, 64, above, -1)
    to_left(own, 0, 64)
    to_right(own, 0, 64)
    to_down(own, 64, 128)
    to_up(own, 64, 128)
    across("x", 0, 64)
    across("y", 64, 128)
    send_line(0, 64, 128, below, 1)
    send_line(0, 64, 128, above, -1)
    to_left(own, 64, 128)
    to_right(own, 64, 128)
    to_down(own, 0, 64)
    to_up(own, 0, 64)
    send_partner(0)
    points = e_ref[...].astype(jnp.float32)
    norms = high_dot(jnp.ones((16, WIDTH), jnp.float32), points * points, ((1,), (1,)))
    one = norms.astype(jnp.bfloat16).astype(jnp.float32)
    two = (norms - one).astype(jnp.bfloat16).astype(jnp.float32)
    three = norms - one - two
    at_row = lax.broadcasted_iota(jnp.int32, norms.shape, 0)
    split = jnp.where(at_row == 0, one, jnp.where(at_row == 1, two, three))
    sd[0, 0:RANK, 0:PTS] = s_ref[...]
    sd[0, RANK : RANK + 16, 0:PTS] = split.astype(jnp.bfloat16)
    eb[0:PTS] = e_ref[...]
    ea[0, 0:PTS] = e_ref[...]
    tests_ref[...] = s_ref[...].astype(jnp.float32).T
    send_side(0, below, 1)
    send_side(0, above, -1)
    send_partner_side(0)
    norms_of_plane(0, 1)
    norms_of_line(0)
    multiply([0], 0, 1, first=True)

    line_on(1, 0, 64, below, 1)
    line_on(7, 0, 64, above, -1)
    arrived(((1, 0), 0))
    to_down((1, 0), 0, 64)
    to_up((1, 0), 0, 64)
    arrived(((3, 0), 0))
    to_down((3, 0), 0, 64)
    to_up((3, 0), 0, 64)
    arrived(((0, 1), 64))
    to_left((0, 1), 64, 128)
    to_right((0, 1), 64, 128)
    arrived(((0, 3), 64))
    to_left((0, 3), 64, 128)
    to_right((0, 3), 64, 128)
    line_on(1, 64, 128, below, 1)
    send_partner(1)
    line_on(7, 64, 128, above, -1)
    send_partner(7)
    arrived(((2, 0), 0))
    to_down((2, 0), 0, 64)
    to_up((2, 0), 0, 64)
    arrived(((0, 2), 64))
    to_left((0, 2), 64, 128)
    to_right((0, 2), 64, 128)
    arrived(((1, 0), 64))
    to_left((1, 0), 64, 128)
    arrived(((0, 1), 0))
    to_down((0, 1), 0, 64)
    side_on(1, below, 1)
    side_on(7, above, -1)
    arrived(((3, 0), 64), ((0, 3), 0))
    norms_of_plane(1, 5)
    multiply([0], 1, 5, first=True)
    norms_of_line(1)
    norms_of_line(7)
    multiply([1, 2], 0, 5)

    line_on(2, 0, 64, below, 1)
    line_on(6, 0, 64, above, -1)
    arrived(((1, 1), 0))
    to_down((1, 1), 0, 64)
    arrived(((3, 3), 0))
    to_up((3, 3), 0, 64)
    arrived(((1, 1), 64))
    to_left((1, 1), 64, 128)
    arrived(((3, 3), 64))
    to_right((3, 3), 64, 128)
    line_on(2, 64, 128, below, 1)
    send_partner(2)
    line_on(6, 64, 128, above, -1)
    send_partner(6)
    arrived(((2, 3), 0))
    to_up((2, 3), 0, 64)
    arrived(((3, 2), 64))
    to_right((3, 2), 64, 128)
    side_on(2, below, 1)
    side_on(6, above, -1)
    arrived(((3, 1), 0), ((3, 1), 64), ((1, 3), 0), ((1, 3), 64), ((2, 0), 64), ((0, 2), 0))
    norms_of_plane(5, 11)
    multiply([0, 1, 2], 5, 11, first=True)
    norms_of_line(2)
    norms_of_line(6)
    multiply([3, 4], 0, 11)

    line_on(3, 0, 64, below, 1)
    arrived(("line", 5, 64))
    send_line(5, 64, 128, above, -1)
    arrived(("line", 3, 64), ("line", 5, 0))
    send_partner(3)
    send_partner(5)
    side_on(3, below, 1)
    arrived(("side", 5))
    send_partner_side(5)
    arrived(((2, 1), 0), ((2, 1), 64), ((2, 3), 64), ((1, 2), 0), ((1, 2), 64), ((3, 2), 0), ((2, 2), 0), ((2, 2), 64))
    norms_of_plane(11, 16)
    multiply([0, 1, 2, 3, 4], 11, 16, first=True)
    norms_of_line(3)
    norms_of_line(5)
    multiply([5, 6], 8, 16)
    arrived(("line", 4, 0), ("line", 4, 64))
    send_partner(4)
    arrived(("side", 4))
    send_partner_side(4)
    multiply([5, 6], 0, 8)

    norms_of_line(4)
    for lo in (12, 8, 4, 0):
        multiply([7], lo, lo + 4)
        for at in reversed(range(max(lo, 1), lo + 4)):
            rs_out[at] = side_by_side(y_acc[at * PTS : (at + 1) * PTS]).astype(PART)
        for at in reversed(range(max(lo, 1), lo + 4)):
            dx, dy = PLANE[at]
            there = PLANE_AT[(-dx % NX, -dy % NY)]
            send(("part", there), rs_out.at[at], rs_in.at[there], plane_peer(dx, dy))

    total = side_by_side(y_acc[0:PTS])
    for at in range(1, 16):
        arrived(("part", at))
        total = total + rs_in[at].astype(jnp.float32)
    sketched = one_above_other(total)
    tests = tests_ref[...]
    products = high_dot(
        jnp.concatenate([tests, sketched], axis=1),
        jnp.concatenate([sketched, tests], axis=1),
        ((0,), (0,)),
    )
    top, bottom = products[:RANK], products[RANK:]
    turned = jnp.concatenate([top[:, RANK:], top[:, :RANK]], axis=1)
    lane = lax.broadcasted_iota(jnp.int32, bottom.shape, 1)
    gram[...] = jnp.where(lane < RANK, bottom, 0.5 * (bottom + turned))

    for copy in copies.values():
        copy.wait_send()
    over = describe("over", gram, g_part, partner)
    back = describe("back", g_sum.at[3], g_sum.at[3], partner)
    stages = []
    for stage, axis, size, landing in ((0, "x", NX, g_x), (1, "y", NY, g_y), (2, "z", NZ, g_z)):
        stages.append((stage, landing, [
            describe((axis, by), g_sum.at[stage], landing.at[by - 1], {axis: shift(axis, by, size)})
            for by in range(1, size)
        ]))

    @pl.when(core == 0)
    def _():
        over.start()
        over.wait_send()
        back.wait_recv()

    @pl.when(core == 1)
    def _():
        over.wait_recv()
        g_sum[0] = gram[...] + g_part[...]
        for stage, landing, group in stages:
            for copy in group:
                copy.start()
            value = g_sum[stage]
            for at, copy in enumerate(group):
                copy.wait_recv()
                value = value + landing[at]
            g_sum[stage + 1] = value
        back.start()
        for _, _, group in stages:
            for copy in group:
                copy.wait_send()
        back.wait_send()

    both = g_sum[3]
    low = jnp.concatenate(inverses_of_cholesky([both[:, :RANK], both[:, RANK:]]), axis=0)
    both_ref[...] = high_dot(low, sketched, ((1,), (1,))) * math.sqrt(PTS * 256)
    assert len(copies) <= N_COPIES


def per_device(embeddings, sketch):
    vmem = pl.BlockSpec(memory_space=pltpu.VMEM)
    pair = (RANK, 2 * RANK)
    both = pl.pallas_call(
        kernel,
        out_shape=jax.ShapeDtypeStruct((2 * RANK, PTS), jnp.float32),
        in_specs=[vmem, vmem],
        out_specs=vmem,
        scratch_shapes=[
            pltpu.VMEM((NZ, 2 * PTS, WIDTH), jnp.bfloat16),
            pltpu.VMEM((16 * PTS, WIDTH), jnp.bfloat16),
            pltpu.VMEM((NZ, RANK + 16, 2 * PTS), jnp.bfloat16),
            pltpu.VMEM((NZ, 8, 2 * PTS), jnp.float32),
            pltpu.VMEM((16 * PTS, 128), jnp.float32),
            pltpu.VMEM((16 * PTS, RANK), jnp.float32),
            pltpu.VMEM((PTS, RANK), jnp.float32),
            pltpu.VMEM((16, PTS // 2, 2 * RANK), PART),
            pltpu.VMEM((16, PTS // 2, 2 * RANK), PART),
            pltpu.VMEM(pair, jnp.float32),
            pltpu.VMEM(pair, jnp.float32),
            pltpu.VMEM((NX - 1, *pair), jnp.float32),
            pltpu.VMEM((NY - 1, *pair), jnp.float32),
            pltpu.VMEM((NZ - 1, *pair), jnp.float32),
            pltpu.VMEM((4, *pair), jnp.float32),
            pltpu.SemaphoreType.DMA((N_COPIES,)),
            pltpu.SemaphoreType.DMA((N_COPIES,)),
        ],
        compiler_params=pltpu.CompilerParams(
            collective_id=0, has_side_effects=True, vmem_limit_bytes=24 << 20
        ),
        name="nystrom",
    )(embeddings, sketch.T)
    return both[:RANK].T, both[RANK:].T


def solution(mesh):
    torus = Mesh(mesh.devices.reshape(NX, 2, NY, NZ), AXES)
    spec = P(AXES, None)
    return jax.shard_map(
        per_device, mesh=torus, in_specs=(spec, spec), out_specs=(spec, spec), check_vma=False
    )
```

time: 61.9 us -> 60.4 us (0.976)
  Pallas kernels: 59.6 us -> 57.3 us
  local copies, waits for them, and re-layouts: 1.4 us -> 2.24 us
    pallas_call x1, Pallas kernels: 59.6 us -> 57.3 us  [per_device(): pl.pallas_call(kernel, out_shape=jax.ShapeDtypeStruct((2 * RANK, PTS), jn...]
    unnamed x0 -> x4, local copies, waits for them, and re-layouts: none -> 1.61 us
    transpose x1, local copies, waits for them, and re-layouts: 1.4 us -> 0.63 us  [per_device(): return (both[:RANK].T, both[RANK:].T)]
where the time goes in v3:
time: 60.4 us; the launch traced here: 60.2 us
  Pallas kernels  57.3 us (95%)
  local copies, waits for them, and re-layouts  2.24 us (4%)
  between operations  0.65 us (1%)
    pallas_call x1, Pallas kernels, per_device(): pl.pallas_call(kernel, out_shape=jax.ShapeDtypeStruct((2 * RANK, PTS), jn...  57.3 us
    unnamed x4, local copies, waits for them, and re-layouts  1.61 us

profile of v3, /device:TPU:1, one launch (start us, length us, event | category | flops | bytes accessed | tf_op | source)
XLA Modules:
  0.0 60.2 jit_solution(8977538921984696412)
XLA Ops:
  0.6 0.0 copy-start
  0.6 0.9 %copy-done = bf16[128,512]{1,0:T(8,128)(2,1)S(1)} copy-done((bf16[128,512]{1,0:T(8,128)(2,1)S(1)}, bf16[128,512]{1,0:T(8,128)(2,1)}, u32[]{:S(2)}) %copy-start) | copy-done | bytes 131096
  1.5 0.0 copy-start.1
  1.5 0.7 %copy-done.1 = bf16[128,64]{0,1:T(8,128)(2,1)S(1)} copy-done((bf16[128,64]{0,1:T(8,128)(2,1)S(1)}, bf16[128,64]{0,1:T(8,128)(2,1)}, u32[]{:S(2)}) %copy-start.1) | copy-done | bytes 16408
  2.3 57.3 %nystrom.1 = f32[128,128]{1,0:T(8,128)S(1)} custom-call(bf16[128,512]{1,0:T(8,128)(2,1)S(1)} %copy-done, bf16[64,128]{1,0:T(8,128)(2,1)S(1)} %bitcast.5), custom_call_target="tpu_custom_call" | custom-call | tf_op jit(solution)/shard_map/nystrom/pallas_call | solution.py:419
  59.6 0.6 %slice_bitcast_fusion = (f32[128,64]{0,1:T(8,128)}, f32[128,64]{0,1:T(8,128)}) fusion(f32[128,128]{1,0:T(8,128)S(1)} %nystrom.1), kind=kLoop, calls=%fused_computation | loop fusion | bytes 131072 | tf_op jit(solution)/shard_map/transpose | solution.py:448
Async XLA Ops:
  0.6 0.9 %copy-start = (bf16[128,512]{1,0:T(8,128)(2,1)S(1)}, bf16[128,512]{1,0:T(8,128)(2,1)}, u32[]{:S(2)}) copy-start(bf16[128,512]{1,0:T(8,128)(2,1)} %e_ref.1) | copy-start | bytes 393220
  1.5 0.7 %copy-start.1 = (bf16[128,64]{0,1:T(8,128)(2,1)S(1)}, bf16[128,64]{0,1:T(8,128)(2,1)}, u32[]{:S(2)}) copy-start(bf16[128,64]{0,1:T(8,128)(2,1)} %param.3) | copy-start | bytes 49156

commit v4 on v3

--- a/solution.py
+++ b/solution.py
@@ -23,8 +23,7 @@
 LINE = [0, 1, 7, 2, 6, 3, 5, 4]
 PLANE_AT = {offset: at for at, offset in enumerate(PLANE)}
 LINE_AT = {offset: at for at, offset in enumerate(LINE)}
-N_COPIES = 128
-PART = jnp.float32
+N_COPIES = 144
 
 
 def high_dot(left, right, dims):
@@ -95,7 +94,7 @@
 
 def kernel(
     e_ref, s_ref, both_ref,
-    ea, eb, sd, naf, nbf, y_acc, tests_ref, rs_out, rs_in, gram, g_part, g_x, g_y, g_z, g_sum,
+    ea, eb, sd, naf, nbf, y_acc, tests_ref, rs_out, rs_in, owned, g_x, g_y, g_z, g_sum,
     send_sem, recv_sem,
 ):
     me = {axis: lax.axis_index(axis) for axis in AXES}
@@ -253,12 +252,13 @@
     sd[0, RANK : RANK + 16, 0:PTS] = split.astype(jnp.bfloat16)
     eb[0:PTS] = e_ref[...]
     ea[0, 0:PTS] = e_ref[...]
-    tests_ref[...] = s_ref[...].astype(jnp.float32).T
+    tests_ref[0] = s_ref[...].astype(jnp.float32).T
     send_side(0, below, 1)
     send_side(0, above, -1)
     send_partner_side(0)
     norms_of_plane(0, 1)
     norms_of_line(0)
+    tests_ref[1] = sd[0, 0:RANK, PTS : 2 * PTS].astype(jnp.float32).T
     multiply([0], 0, 1, first=True)
 
     line_on(1, 0, 64, below, 1)
@@ -346,35 +346,29 @@
     send_partner_side(4)
     multiply([5, 6], 0, 8)
 
+    gathers = list(copies.values())
     norms_of_line(4)
     for lo in (12, 8, 4, 0):
         multiply([7], lo, lo + 4)
-        for at in reversed(range(max(lo, 1), lo + 4)):
-            rs_out[at] = side_by_side(y_acc[at * PTS : (at + 1) * PTS]).astype(PART)
-        for at in reversed(range(max(lo, 1), lo + 4)):
+        for at in reversed(range(lo, lo + 4)):
+            rs_out[at] = side_by_side(y_acc[at * PTS : (at + 1) * PTS])
+        group = []
+        for at in reversed(range(lo, lo + 4)):
             dx, dy = PLANE[at]
             there = PLANE_AT[(-dx % NX, -dy % NY)]
-            send(("part", there), rs_out.at[at], rs_in.at[there], plane_peer(dx, dy))
-
-    total = side_by_side(y_acc[0:PTS])
-    for at in range(1, 16):
-        arrived(("part", at))
-        total = total + rs_in[at].astype(jnp.float32)
-    sketched = one_above_other(total)
-    tests = tests_ref[...]
-    products = high_dot(
-        jnp.concatenate([tests, sketched], axis=1),
-        jnp.concatenate([sketched, tests], axis=1),
-        ((0,), (0,)),
-    )
-    top, bottom = products[:RANK], products[RANK:]
-    turned = jnp.concatenate([top[:, RANK:], top[:, :RANK]], axis=1)
-    lane = lax.broadcasted_iota(jnp.int32, bottom.shape, 1)
-    gram[...] = jnp.where(lane < RANK, bottom, 0.5 * (bottom + turned))
-
-    for copy in copies.values():
-        copy.wait_send()
-    over = describe("over", gram, g_part, partner)
+            for c in range(2):
+                to = partner if at == 0 else {**plane_peer(dx, dy), "core": 1}
+                if at > 0 or c == 0:
+                    group.append((c, describe(("part", c, there), rs_out.at[at], rs_in.at[c, there], to)))
+        for c in range(2):
+
+            @pl.when(core == c)
+            def _():
+                for whose, copy in group:
+                    if whose == c:
+                        copy.start()
+
+    to_partner = describe("rows", owned.at[0], owned.at[0], partner)
     back = describe("back", g_sum.at[3], g_sum.at[3], partner)
     stages = []
     for stage, axis, size, landing in ((0, "x", NX, g_x), (1, "y", NY, g_y), (2, "z", NZ, g_z)):
@@ -383,16 +377,40 @@
             for by in range(1, size)
         ]))
 
+    def given(c):
+        return [copies[("part", c, at)] for at in range(1 if c else 0, 16)]
+
     @pl.when(core == 0)
     def _():
-        over.start()
-        over.wait_send()
+        for copy in given(0):
+            copy.wait_send()
+        to_partner.wait_recv()
         back.wait_recv()
 
     @pl.when(core == 1)
     def _():
-        over.wait_recv()
-        g_sum[0] = gram[...] + g_part[...]
+        totals = []
+        for c in range(2):
+            total = None if c == 0 else rs_out[0]
+            for at in range(1 if c else 0, 16):
+                copies[("part", c, at)].wait_recv()
+                term = rs_in[c, at]
+                total = term if total is None else total + term
+            totals.append(total)
+            owned[c] = total
+            if c == 0:
+                to_partner.start()
+        sketched = jnp.concatenate([one_above_other(total) for total in totals], axis=0)
+        tests = jnp.concatenate([tests_ref[1], tests_ref[0]], axis=0)
+        products = high_dot(
+            jnp.concatenate([tests, sketched], axis=1),
+            jnp.concatenate([sketched, tests], axis=1),
+            ((0,), (0,)),
+        )
+        top, bottom = products[:RANK], products[RANK:]
+        turned = jnp.concatenate([top[:, RANK:], top[:, :RANK]], axis=1)
+        lane = lax.broadcasted_iota(jnp.int32, bottom.shape, 1)
+        g_sum[0] = jnp.where(lane < RANK, bottom, 0.5 * (bottom + turned))
         for stage, landing, group in stages:
             for copy in group:
                 copy.start()
@@ -405,8 +423,14 @@
         for _, _, group in stages:
             for copy in group:
                 copy.wait_send()
+        for copy in given(1):
+            copy.wait_send()
+        to_partner.wait_send()
         back.wait_send()
 
+    for copy in gathers:
+        copy.wait_send()
+    sketched = one_above_other(owned[core])
     both = g_sum[3]
     low = jnp.concatenate(inverses_of_cholesky([both[:, :RANK], both[:, RANK:]]), axis=0)
     both_ref[...] = high_dot(low, sketched, ((1,), (1,))) * math.sqrt(PTS * 256)
@@ -428,11 +452,10 @@
             pltpu.VMEM((NZ, 8, 2 * PTS), jnp.float32),
             pltpu.VMEM((16 * PTS, 128), jnp.float32),
             pltpu.VMEM((16 * PTS, RANK), jnp.float32),
-            pltpu.VMEM((PTS, RANK), jnp.float32),
-            pltpu.VMEM((16, PTS // 2, 2 * RANK), PART),
-            pltpu.VMEM((16, PTS // 2, 2 * RANK), PART),
-            pltpu.VMEM(pair, jnp.float32),
-            pltpu.VMEM(pair, jnp.float32),
+            pltpu.VMEM((2, PTS, RANK), jnp.float32),
+            pltpu.VMEM((16, PTS // 2, 2 * RANK), jnp.float32),
+            pltpu.VMEM((2, 16, PTS // 2, 2 * RANK), jnp.float32),
+            pltpu.VMEM((2, PTS // 2, 2 * RANK), jnp.float32),
             pltpu.VMEM((NX - 1, *pair), jnp.float32),
             pltpu.VMEM((NY - 1, *pair), jnp.float32),
             pltpu.VMEM((NZ - 1, *pair), jnp.float32),

time: 60.4 us -> 59 us (0.977)
  Pallas kernels: 57.3 us -> 56 us
    pallas_call x1, Pallas kernels: 57.3 us -> 56 us  [per_device(): pl.pallas_call(kernel, out_shape=jax.ShapeDtypeStruct((2 * RANK, PTS), jn...]
where the time goes in v4:
time: 59 us; the launch traced here: 58.9 us
  Pallas kernels  56 us (95%)
  local copies, waits for them, and re-layouts  2.24 us (4%)
  between operations  0.65 us (1%)
    pallas_call x1, Pallas kernels, per_device(): pl.pallas_call(kernel, out_shape=jax.ShapeDtypeStruct((2 * RANK, PTS), jn...  56 us
    unnamed x4, local copies, waits for them, and re-layouts  1.61 us

profile of v4, /device:TPU:1, one launch (start us, length us, event | category | flops | bytes accessed | tf_op | source)
XLA Modules:
  0.0 58.9 jit_solution(7142915247485650830)
XLA Ops:
  0.6 0.0 copy-start
  0.6 0.9 %copy-done = bf16[128,512]{1,0:T(8,128)(2,1)S(1)} copy-done((bf16[128,512]{1,0:T(8,128)(2,1)S(1)}, bf16[128,512]{1,0:T(8,128)(2,1)}, u32[]{:S(2)}) %copy-start) | copy-done | bytes 131096
  1.5 0.0 copy-start.1
  1.5 0.7 %copy-done.1 = bf16[128,64]{0,1:T(8,128)(2,1)S(1)} copy-done((bf16[128,64]{0,1:T(8,128)(2,1)S(1)}, bf16[128,64]{0,1:T(8,128)(2,1)}, u32[]{:S(2)}) %copy-start.1) | copy-done | bytes 16408
  2.3 56.0 %nystrom.1 = f32[128,128]{1,0:T(8,128)S(1)} custom-call(bf16[128,512]{1,0:T(8,128)(2,1)S(1)} %copy-done, bf16[64,128]{1,0:T(8,128)(2,1)S(1)} %bitcast.5), custom_call_target="tpu_custom_call" | custom-call | tf_op jit(solution)/shard_map/nystrom/pallas_call | solution.py:443
  58.2 0.6 %slice_bitcast_fusion = (f32[128,64]{0,1:T(8,128)}, f32[128,64]{0,1:T(8,128)}) fusion(f32[128,128]{1,0:T(8,128)S(1)} %nystrom.1), kind=kLoop, calls=%fused_computation | loop fusion | bytes 131072 | tf_op jit(solution)/shard_map/transpose | solution.py:471
Async XLA Ops:
  0.6 0.9 %copy-start = (bf16[128,512]{1,0:T(8,128)(2,1)S(1)}, bf16[128,512]{1,0:T(8,128)(2,1)}, u32[]{:S(2)}) copy-start(bf16[128,512]{1,0:T(8,128)(2,1)} %e_ref.1) | copy-start | bytes 393220
  1.5 0.7 %copy-start.1 = (bf16[128,64]{0,1:T(8,128)(2,1)S(1)}, bf16[128,64]{0,1:T(8,128)(2,1)}, u32[]{:S(2)}) copy-start(bf16[128,64]{0,1:T(8,128)(2,1)} %param.3) | copy-start | bytes 49156

commit v5 on v4

--- a/solution.py
+++ b/solution.py
@@ -337,14 +337,13 @@
     arrived(((2, 1), 0), ((2, 1), 64), ((2, 3), 64), ((1, 2), 0), ((1, 2), 64), ((3, 2), 0), ((2, 2), 0), ((2, 2), 64))
     norms_of_plane(11, 16)
     multiply([0, 1, 2, 3, 4], 11, 16, first=True)
-    norms_of_line(3)
-    norms_of_line(5)
-    multiply([5, 6], 8, 16)
     arrived(("line", 4, 0), ("line", 4, 64))
     send_partner(4)
     arrived(("side", 4))
     send_partner_side(4)
-    multiply([5, 6], 0, 8)
+    norms_of_line(3)
+    norms_of_line(5)
+    multiply([5, 6], 0, 16)
 
     gathers = list(copies.values())
     norms_of_line(4)

time: 59 us -> 59 us (level)
  no operation moved by 1% of the time
where the time goes in v5:
time: 59 us; the launch traced here: 58.8 us
  Pallas kernels  55.9 us (95%)
  local copies, waits for them, and re-layouts  2.24 us (4%)
  between operations  0.65 us (1%)
    pallas_call x1, Pallas kernels, per_device(): pl.pallas_call(kernel, out_shape=jax.ShapeDtypeStruct((2 * RANK, PTS), jn...  55.9 us
    unnamed x4, local copies, waits for them, and re-layouts  1.61 us

profile of v5, /device:TPU:1, one launch (start us, length us, event | category | flops | bytes accessed | tf_op | source)
XLA Modules:
  0.0 58.8 jit_solution(2727959554941207913)
XLA Ops:
  0.6 0.0 copy-start
  0.6 0.9 %copy-done = bf16[128,512]{1,0:T(8,128)(2,1)S(1)} copy-done((bf16[128,512]{1,0:T(8,128)(2,1)S(1)}, bf16[128,512]{1,0:T(8,128)(2,1)}, u32[]{:S(2)}) %copy-start) | copy-done | bytes 131096
  1.5 0.0 copy-start.1
  1.5 0.7 %copy-done.1 = bf16[128,64]{0,1:T(8,128)(2,1)S(1)} copy-done((bf16[128,64]{0,1:T(8,128)(2,1)S(1)}, bf16[128,64]{0,1:T(8,128)(2,1)}, u32[]{:S(2)}) %copy-start.1) | copy-done | bytes 16408
  2.3 55.9 %nystrom.1 = f32[128,128]{1,0:T(8,128)S(1)} custom-call(bf16[128,512]{1,0:T(8,128)(2,1)S(1)} %copy-done, bf16[64,128]{1,0:T(8,128)(2,1)S(1)} %bitcast.5), custom_call_target="tpu_custom_call" | custom-call | tf_op jit(solution)/shard_map/nystrom/pallas_call | solution.py:442
  58.2 0.6 %slice_bitcast_fusion = (f32[128,64]{0,1:T(8,128)}, f32[128,64]{0,1:T(8,128)}) fusion(f32[128,128]{1,0:T(8,128)S(1)} %nystrom.1), kind=kLoop, calls=%fused_computation | loop fusion | bytes 131072 | tf_op jit(solution)/shard_map/transpose | solution.py:470
Async XLA Ops:
  0.6 0.9 %copy-start = (bf16[128,512]{1,0:T(8,128)(2,1)S(1)}, bf16[128,512]{1,0:T(8,128)(2,1)}, u32[]{:S(2)}) copy-start(bf16[128,512]{1,0:T(8,128)(2,1)} %e_ref.1) | copy-start | bytes 393220
  1.5 0.7 %copy-start.1 = (bf16[128,64]{0,1:T(8,128)(2,1)S(1)}, bf16[128,64]{0,1:T(8,128)(2,1)}, u32[]{:S(2)}) copy-start(bf16[128,64]{0,1:T(8,128)(2,1)} %param.3) | copy-start | bytes 49156
